TPU v7x, 32 devices: a whole 2x2x4 slice. The times are simulated.
32 devices in a mesh: rows: 16 (over z, y, x), sub: 2 (over core).
Axes of the slice: x: 2, y: 2, z: 4, core: 2. Of those that a mesh axis runs over, the one named last changes fastest.
Arguments:
- matrix: float32 [4096, 384], P(('rows', 'sub')), as said below
- grad_out: float32 [4096, 384], P(('rows', 'sub')), as said below
- grad_factor: float32 [384, 384], replicated, may hold values from -6 to 6
Outputs:
- grad_matrix: float32 [4096, 384], P(('rows', 'sub'))
Inputs may be any that keep to these rules, and one draw needn't show every extreme that they name: `matrix`: entries at most of order 1 / sqrt(4096), with a scale that varies by row and by column. `grad_out`: entries of order 0.01.
All inputs are finite; a program needn't handle non-finite values.
Results may differ from a plain program's by a relative error of at most 0.0004.
Values sent between devices are 32-bit elements; how exact they have to be, the bound alone decides.
A program may use at most 64 MiB of HBM per device.

v0:
```python
import functools

import jax
import jax.numpy as jnp
from jax import lax
from jax.experimental import pallas as pl
from jax.experimental.pallas import tpu as pltpu
from jax.sharding import PartitionSpec as P

LANES = 128
PANEL = 16
shift_frac = 0.02
VMEM_LIMIT = 56 * 1024 * 1024


def dot(left, right, dims=((1,), (0,))):
    return lax.dot_general(
        left, right, (dims, ((), ())), precision=lax.Precision.HIGHEST, preferred_element_type=jnp.float32
    )


def halves(value):
    high = value.astype(jnp.bfloat16)
    return high, (value - high.astype(jnp.float32)).astype(jnp.bfloat16)


def dot3(left, right, dims=((1,), (0,))):
    (left_high, left_low), (right_high, right_low) = halves(left), halves(right)

    def product(a, b):
        return lax.dot_general(a, b, (dims, ((), ())), preferred_element_type=jnp.float32)

    return product(left_high, right_high) + (product(left_high, right_low) + product(left_low, right_high))


def dot3_tn(left, right):
    return dot3(left, right, ((0,), (0,)))


def dot3_nt(left, right):
    return dot3(left, right, ((1,), (1,)))


def dot_tn(left, right):
    return dot(left, right, ((0,), (0,)))


def dot_nt(left, right):
    return dot(left, right, ((1,), (1,)))


def upper_pairs(count):
    return [(i, j) for i in range(count) for j in range(i, count)]


def block(index):
    return pl.ds(index * LANES, LANES)


def iotas(shape):
    return lax.broadcasted_iota(jnp.int32, shape, 0), lax.broadcasted_iota(jnp.int32, shape, 1)


def piece_rows(rows, devices):
    share = -(-rows // devices)
    return -(-share // 8) * 8


class Summer:
    def __init__(self, counts, rows):
        self.counts, self.used = counts, rows
        self.devices = counts[0] * counts[1]
        self.piece = piece_rows(rows, self.devices)
        self.owners = -(-rows // self.piece)
        self.rows = self.owners * self.piece

    def scratch(self):
        return [
            pltpu.VMEM((self.rows, LANES), jnp.float32),
            pltpu.VMEM((self.devices - 1, self.piece, LANES), jnp.float32),
            pltpu.VMEM((self.rows, LANES), jnp.float32),
            pltpu.SemaphoreType.DMA((4,)),
        ]

    def bind(self, me, part, inbox, total, sems):
        self.me, self.part, self.inbox, self.total, self.sems = me, part, inbox, total, sems
        return self

    def peer(self, offset):
        return lax.rem(self.me + offset, self.devices)

    def place(self, device):
        return (device // self.counts[1], lax.rem(device, self.counts[1]))

    def rows_of(self, device):
        return pl.ds(pl.multiple_of(device * self.piece, 8), self.piece)

    def is_owner(self, device, action):
        if self.owners == self.devices:
            action()
        else:
            pl.when(device < self.owners)(action)

    def greet(self):
        barrier = pltpu.get_barrier_semaphore()

        def signal(offset, carry):
            pl.semaphore_signal(
                barrier, inc=1, device_id=self.place(self.peer(offset)), device_id_type=pl.DeviceIdType.MESH
            )
            return carry

        lax.fori_loop(1, self.devices, signal, 0)

    def greeted(self):
        pl.semaphore_wait(pltpu.get_barrier_semaphore(), self.devices - 1)

    def outgoing(self, offset):
        peer = self.peer(offset)
        return pltpu.make_async_remote_copy(
            src_ref=self.part.at[self.rows_of(peer)],
            dst_ref=self.inbox.at[offset - 1],
            send_sem=self.sems.at[0],
            recv_sem=self.sems.at[1],
            device_id=self.place(peer),
            device_id_type=pl.DeviceIdType.MESH,
        )

    def spread(self, offset):
        mine = self.total.at[self.rows_of(self.me)]
        return pltpu.make_async_remote_copy(
            src_ref=mine,
            dst_ref=mine,
            send_sem=self.sems.at[2],
            recv_sem=self.sems.at[3],
            device_id=self.place(self.peer(offset)),
            device_id_type=pl.DeviceIdType.MESH,
        )

    def each_peer(self, action):
        def step(offset, carry):
            action(offset)
            return carry

        lax.fori_loop(1, self.devices, step, 0)

    def start(self):
        if self.rows > self.used:
            spare = self.rows - self.used
            self.part[pl.ds(self.used, spare), :] = jnp.zeros((spare, LANES), jnp.float32)
        self.each_peer(lambda offset: self.is_owner(self.peer(offset), lambda: self.outgoing(offset).start()))

    def reduce(self):
        def owned():
            pltpu.make_async_copy(self.inbox, self.inbox, self.sems.at[1]).wait()
            mine = self.rows_of(self.me)
            summed = self.part[mine, :]
            for slot in range(self.devices - 1):
                summed = summed + self.inbox[slot]
            self.total[mine, :] = summed
            self.each_peer(lambda offset: self.spread(offset).start())

        self.is_owner(self.me, owned)

    def wait_rows(self, rows):
        view = self.total.at[pl.ds(0, rows)]
        pltpu.make_async_copy(view, view, self.sems.at[3]).wait()

    def finish(self):
        if self.owners == self.devices:
            self.wait_rows(self.rows - self.piece)
        else:
            pl.when(self.me < self.owners)(lambda: self.wait_rows(self.rows - self.piece))
            pl.when(self.me >= self.owners)(lambda: self.wait_rows(self.rows))
        self.each_peer(lambda offset: self.is_owner(self.peer(offset), lambda: self.outgoing(offset).wait_send()))
        self.is_owner(self.me, lambda: self.each_peer(lambda offset: self.spread(offset).wait_send()))


def store_gram(part, source, pairs):
    for index, (i, j) in enumerate(pairs):
        part[block(index), :] = dot_tn(source[:, block(i)], source[:, block(j)])


def factor_block(work):
    sub, lane = iotas((PANEL, LANES))

    def step(group, carry):
        top = group * PANEL
        rows = pl.ds(pl.multiple_of(top, PANEL), PANEL)
        waiting, source = carry
        turn = lax.rem(LANES - top, LANES)
        others = work[...] - dot_tn(waiting, source)
        ahead = pltpu.roll(waiting, turn, 1)[:, 0:PANEL]
        panel = work[rows, :] - dot_tn(ahead, source)
        left, right = panel[:, 0:LANES], panel[:, LANES:]
        rolled = pltpu.roll(left, turn, 1)
        cols = [jnp.broadcast_to(rolled[:, k : k + 1], (PANEL, LANES)) for k in range(PANEL)]
        scale = jnp.zeros((PANEL, LANES), jnp.float32)
        for k in range(PANEL):
            root = lax.rsqrt(cols[k][k : k + 1, :])
            scale = jnp.where(sub == k, root, scale)
            factor = jnp.where(sub > k, cols[k] * root, 0.0)
            for later in range(k + 1, PANEL):
                cols[later] = cols[later] - factor * (cols[later][k : k + 1, :] * root)
            left = left - factor * (left[k : k + 1, :] * root)
            right = right - factor * (right[k : k + 1, :] * root)
        left = jnp.where(lane >= top + sub, left * scale, 0.0)
        right = right * scale
        both = jnp.concatenate([left, right], axis=1)
        below = jnp.where(lane >= top + PANEL, left, 0.0)
        work[...] = others
        work[rows, :] = both
        return below, both

    none = jnp.zeros((PANEL, LANES), jnp.float32), jnp.zeros((PANEL, 2 * LANES), jnp.float32)
    lax.fori_loop(0, LANES // PANEL, step, none)


def factor_all(width, gram, work, upper, inverse, after_block=lambda b: None):
    pairs = upper_pairs(width)
    size = width * LANES
    rate = shift_frac / size
    row, lane = iotas((LANES, LANES))
    same = row == lane
    trace = jnp.float32(0.0)
    for index, (i, j) in enumerate(pairs):
        if i == j:
            trace = trace + jnp.sum(jnp.where(same, gram[block(index), :], 0.0))
    shift = rate * trace
    eye = jnp.where(same, 1.0, 0.0).astype(jnp.float32)
    zero = jnp.zeros((LANES, LANES), jnp.float32)
    for index, (i, j) in enumerate(pairs):
        piece = gram[block(index), :]
        upper[block(i), block(j)] = piece + shift * eye if i == j else piece
        if i != j:
            upper[block(j), block(i)] = zero
            inverse[block(i), block(j)] = zero
    for b in range(width):
        work[:, pl.ds(0, LANES)] = upper[block(b), block(b)]
        work[:, pl.ds(LANES, LANES)] = eye
        factor_block(work)
        upper[block(b), block(b)] = work[:, pl.ds(0, LANES)]
        inv = work[:, pl.ds(LANES, LANES)]
        inverse[block(b), block(b)] = inv
        for j in range(b + 1, width):
            upper[block(b), block(j)] = dot(inv, upper[block(b), block(j)])
        for i in range(b + 1, width):
            for j in range(i, width):
                upper[block(i), block(j)] = upper[block(i), block(j)] - dot_tn(
                    upper[block(b), block(i)], upper[block(b), block(j)]
                )
        for j in range(b):
            acc = zero
            for k in range(j, b):
                acc = acc + dot_tn(upper[block(k), block(b)], inverse[block(k), block(j)])
            inverse[block(b), block(j)] = -dot(inv, acc)
        after_block(b)


def gram_grad(upper, inverse, total_grad, rate):
    row, lane = iotas(total_grad.shape)
    lower_grad = jnp.where(row >= lane, total_grad.T, 0.0)
    product = dot3(upper, lower_grad)
    phi = jnp.where(row > lane, product, jnp.where(row == lane, 0.5 * product, 0.0))
    sandwich = dot3(dot3_tn(inverse, phi), inverse)
    result = 0.5 * (sandwich + sandwich.T)
    trace = jnp.sum(jnp.where(row == lane, result, 0.0))
    return result + jnp.where(row == lane, rate * trace, 0.0)


def whole_kernel(counts, width, matrix, q_grad, grad_factor, out, *scratch):
    gram_sum, later_sum, cross_sum = scratch[0:4], scratch[4:8], scratch[8:12]
    work, upper1, inverse1, upper2, inverse2, current, square, held = scratch[12:]
    me = lax.axis_index("rows") * counts[1] + lax.axis_index("sub")
    pairs = upper_pairs(width)
    used = len(pairs) * LANES
    rate = shift_frac / (width * LANES)
    first = Summer(counts, used).bind(me, *gram_sum)
    second = Summer(counts, used).bind(me, *later_sum)
    cross = Summer(counts, width * width * LANES).bind(me, *cross_sum)

    first.greet()
    store_gram(first.part, matrix, pairs)
    first.greeted()
    first.start()
    first.reduce()
    first.finish()
    factor_all(width, first.total, work, upper1, inverse1)
    current[...] = dot_nt(matrix[...], inverse1[...])

    store_gram(second.part, current, pairs)
    second.start()
    for i in range(width):
        for j in range(width):
            cross.part[block(i * width + j), :] = dot_tn(current[:, block(i)], q_grad[:, block(j)])
    held[...] = dot3_nt(grad_factor[...], upper1[...])
    second.reduce()
    second.finish()
    cross.start()

    def after_block(b):
        if b == width - 2:
            cross.reduce()

    factor_all(width, second.total, work, upper2, inverse2, after_block)
    factor1 = dot3_tn(upper2[...], grad_factor[...])
    moved = dot3(q_grad[...], inverse2[...])
    cross.finish()
    for i in range(width):
        for j in range(width):
            square[block(i), block(j)] = cross.total[block(i * width + j), :]
    turned = dot3(square[...], inverse2[...])
    total2 = held[...] - dot3(inverse2[...], turned)
    grad2 = gram_grad(upper2[...], inverse2[...], total2, rate)
    for index, (i, j) in enumerate(pairs):
        piece = second.total[block(index), :]
        square[block(i), block(j)] = piece
        if i != j:
            square[block(j), block(i)] = piece.T
    crossed1 = turned + 2.0 * dot3(square[...], grad2)
    total1 = factor1 - dot3(crossed1, inverse1[...])
    grad1 = gram_grad(upper1[...], inverse1[...], total1, rate)
    middle = moved + 2.0 * dot3(current[...], grad2)
    out[...] = dot3(middle, inverse1[...]) + 2.0 * dot3(matrix[...], grad1)


def per_device(counts, matrix, grad_out, grad_factor):
    rows, size = matrix.shape
    width = size // LANES
    used = len(upper_pairs(width)) * LANES
    vmem = pl.BlockSpec(memory_space=pltpu.VMEM)
    square = pltpu.VMEM((size, size), jnp.float32)
    tall = pltpu.VMEM((rows, size), jnp.float32)
    work = pltpu.VMEM((LANES, 2 * LANES), jnp.float32)
    sums = (
        Summer(counts, used).scratch() + Summer(counts, used).scratch() + Summer(counts, width * size).scratch()
    )
    return pl.pallas_call(
        functools.partial(whole_kernel, counts, width),
        out_shape=jax.ShapeDtypeStruct((rows, size), jnp.float32),
        in_specs=[vmem] * 3,
        out_specs=vmem,
        scratch_shapes=sums + [work] + [square] * 4 + [tall, square, square],
        compiler_params=pltpu.CompilerParams(
            vmem_limit_bytes=VMEM_LIMIT, collective_id=0, has_side_effects=True
        ),
    )(matrix, grad_out, grad_factor)


def solution(mesh):
    counts = (mesh.shape["rows"], mesh.shape["sub"])
    placed = (P(("rows", "sub"), None), P(("rows", "sub"), None), P())
    return jax.shard_map(
        functools.partial(per_device, counts),
        mesh=mesh,
        in_specs=placed,
        out_specs=P(("rows", "sub"), None),
        check_vma=False,
    )
```

profile of v0, /device:TPU:29, one launch (start us, length us, event | category | flops | bytes accessed | tf_op | source)
XLA Modules:
  0.0 109.3 jit_solution(17113473755647507737)
XLA Ops:
  0.0 107.7 %shard_map.37 = f32[128,384]{1,0:T(8,128)} custom-call(f32[128,384]{1,0:T(8,128)} %matrix.1, f32[128,384]{1,0:T(8,128)} %q_grad.1, f32[384,384]{1,0:T(8,128)} %grad_factor.1), custom_call_target="tpu_custom_call" | custom-call | tf_op jit(solution)/shard_map/pallas_call | solution.py:338
  107.7 1.6 %copy.5 = f32[128,384]{1,0:T(8,128)} copy(f32[128,384]{1,0:T(8,128)} %shard_map.37) | data formatting | bytes 393216
where the time goes:
time: 109 us
  Pallas kernels  108 us (99%)
  local copies, waits for them, and re-layouts  1.62 us (1%)
    pallas_call x1, Pallas kernels, per_device(): pl.pallas_call(functools.partial(whole_kernel, counts, width), out_shape=...  108 us

commit v1 on v0

--- a/solution.py
+++ b/solution.py
@@ -9,6 +9,7 @@
 
 LANES = 128
 PANEL = 16
+SUBLANES = 8
 shift_frac = 0.02
 VMEM_LIMIT = 56 * 1024 * 1024
 
@@ -181,39 +182,72 @@
         part[block(index), :] = dot_tn(source[:, block(i)], source[:, block(j)])
 
 
+def thirds(value):
+    high = value.astype(jnp.bfloat16)
+    rest = value - high.astype(jnp.float32)
+    middle = rest.astype(jnp.bfloat16)
+    return high, middle, (rest - middle.astype(jnp.float32)).astype(jnp.bfloat16)
+
+
+def packed_tn(left, right):
+    (a, b, c), (d, e, f) = thirds(left), thirds(right)
+    tall = jnp.concatenate([a, a, b, a, c, b], axis=0)
+    wide = jnp.concatenate([d, e, d, f, d, e], axis=0)
+    return lax.dot_general(tall, wide, (((0,), (0,)), ((), ())), preferred_element_type=jnp.float32)
+
+
+def eliminate(pieces, first):
+    sub, lane = iotas((SUBLANES, LANES))
+    cols = [
+        [jnp.broadcast_to(piece[0][:, first + k : first + k + 1], (SUBLANES, LANES)) for piece in pieces]
+        for k in range(PANEL)
+    ]
+    roots = []
+    for k in range(PANEL):
+        own, at = k // SUBLANES, k % SUBLANES
+        root = lax.rsqrt(cols[k][own][at : at + 1, :])
+        roots.append(root)
+        factors = {}
+        for i in range(own, len(pieces)):
+            factor = cols[k][i] * root
+            if i > own:
+                factors[i] = factor
+            elif at < SUBLANES - 1:
+                factors[i] = jnp.where(sub > at, factor, 0.0)
+        for later in range(k + 1, PANEL):
+            value = cols[later][own][at : at + 1, :] * root
+            for i, factor in factors.items():
+                cols[later][i] = cols[later][i] - factor * value
+        for tile in range(2):
+            row = pieces[own][tile][at : at + 1, :] * root
+            for i, factor in factors.items():
+                pieces[i][tile] = pieces[i][tile] - factor * row
+    for own in range(PANEL // SUBLANES):
+        scale = jnp.broadcast_to(roots[own * SUBLANES], (SUBLANES, LANES))
+        for at in range(1, SUBLANES):
+            scale = jnp.where(sub == at, roots[own * SUBLANES + at], scale)
+        kept = lane >= first + own * SUBLANES + sub
+        pieces[own][0] = jnp.where(kept, pieces[own][0] * scale, 0.0)
+        pieces[own][1] = pieces[own][1] * scale
+
+
 def factor_block(work):
-    sub, lane = iotas((PANEL, LANES))
-
-    def step(group, carry):
-        top = group * PANEL
-        rows = pl.ds(pl.multiple_of(top, PANEL), PANEL)
-        waiting, source = carry
-        turn = lax.rem(LANES - top, LANES)
-        others = work[...] - dot_tn(waiting, source)
-        ahead = pltpu.roll(waiting, turn, 1)[:, 0:PANEL]
-        panel = work[rows, :] - dot_tn(ahead, source)
-        left, right = panel[:, 0:LANES], panel[:, LANES:]
-        rolled = pltpu.roll(left, turn, 1)
-        cols = [jnp.broadcast_to(rolled[:, k : k + 1], (PANEL, LANES)) for k in range(PANEL)]
-        scale = jnp.zeros((PANEL, LANES), jnp.float32)
-        for k in range(PANEL):
-            root = lax.rsqrt(cols[k][k : k + 1, :])
-            scale = jnp.where(sub == k, root, scale)
-            factor = jnp.where(sub > k, cols[k] * root, 0.0)
-            for later in range(k + 1, PANEL):
-                cols[later] = cols[later] - factor * (cols[later][k : k + 1, :] * root)
-            left = left - factor * (left[k : k + 1, :] * root)
-            right = right - factor * (right[k : k + 1, :] * root)
-        left = jnp.where(lane >= top + sub, left * scale, 0.0)
-        right = right * scale
+    step, count = 2 * PANEL, PANEL // SUBLANES
+    for top in range(0, LANES, step):
+        pieces = []
+        for row in range(top, top + step, SUBLANES):
+            pieces.append([work[row : row + SUBLANES, 0:LANES], work[row : row + SUBLANES, LANES : 2 * LANES]])
+        eliminate(pieces, top)
+        done, pieces = pieces[:count], pieces[count:]
+        eliminate(pieces, top + PANEL)
+        done = done + pieces
+        left = jnp.concatenate([piece[0] for piece in done], axis=0)
+        right = jnp.concatenate([piece[1] for piece in done], axis=0)
         both = jnp.concatenate([left, right], axis=1)
-        below = jnp.where(lane >= top + PANEL, left, 0.0)
-        work[...] = others
-        work[rows, :] = both
-        return below, both
-
-    none = jnp.zeros((PANEL, LANES), jnp.float32), jnp.zeros((PANEL, 2 * LANES), jnp.float32)
-    lax.fori_loop(0, LANES // PANEL, step, none)
+        work[top : top + step, :] = both
+        below = top + step
+        if below < LANES:
+            work[below:, :] = work[below:, :] - packed_tn(left, both)[below:, :]
 
 
 def factor_all(width, gram, work, upper, inverse, after_block=lambda b: None):

time: 109 us -> 101 us (0.927)
  Pallas kernels: 108 us -> 99.5 us
    pallas_call x1, Pallas kernels: 108 us -> 99.5 us  [per_device(): pl.pallas_call(functools.partial(whole_kernel, counts, width), out_shape=...]
where the time goes in v1:
time: 101 us
  Pallas kernels  99.5 us (99%)
  local copies, waits for them, and re-layouts  1.62 us (2%)
    pallas_call x1, Pallas kernels, per_device(): pl.pallas_call(functools.partial(whole_kernel, counts, width), out_shape=...  99.5 us

profile of v1, /device:TPU:29, one launch (start us, length us, event | category | flops | bytes accessed | tf_op | source)
XLA Modules:
  0.0 101.1 jit_solution(15100695009803631574)
XLA Ops:
  0.0 99.5 %shard_map.37 = f32[128,384]{1,0:T(8,128)} custom-call(f32[128,384]{1,0:T(8,128)} %matrix.1, f32[128,384]{1,0:T(8,128)} %q_grad.1, f32[384,384]{1,0:T(8,128)} %grad_factor.1), custom_call_target="tpu_custom_call" | custom-call | tf_op jit(solution)/shard_map/pallas_call | solution.py:372
  99.5 1.6 %copy.5 = f32[128,384]{1,0:T(8,128)} copy(f32[128,384]{1,0:T(8,128)} %shard_map.37) | data formatting | bytes 393216

commit v2 on v1

v2 whole, which is shorter than its diff:
```python
import functools

import jax
import jax.numpy as jnp
from jax import lax
from jax.experimental import pallas as pl
from jax.experimental.pallas import tpu as pltpu
from jax.sharding import PartitionSpec as P

LANES = 128
PANEL = 16
SUBLANES = 8
shift_frac = 0.02
VMEM_LIMIT = 56 * 1024 * 1024


NN, NT, TN = ((1,), (0,)), ((1,), (1,)), ((0,), (0,))


def halves(value):
    high = value.astype(jnp.bfloat16)
    return high, (value - high.astype(jnp.float32)).astype(jnp.bfloat16)


def thirds(value):
    high = value.astype(jnp.bfloat16)
    rest = value - high.astype(jnp.float32)
    middle = rest.astype(jnp.bfloat16)
    return high, middle, (rest - middle.astype(jnp.float32)).astype(jnp.bfloat16)


def joined(left, right, dims):
    (left_axis,), (right_axis,) = dims
    left, right = jnp.concatenate(left, axis=left_axis), jnp.concatenate(right, axis=right_axis)
    return lax.dot_general(left, right, (dims, ((), ())), preferred_element_type=jnp.float32)


def dot6(left, right, dims=NN):
    (a, b, c), (d, e, f) = thirds(left), thirds(right)
    return joined([a, a, b, a, c, b], [d, e, d, f, d, e], dims)


def dot3(left, right, dims=NN):
    (a, b), (d, e) = halves(left), halves(right)
    return joined([a, a, b], [d, e, d], dims)


def upper_pairs(count):
    return [(i, j) for i in range(count) for j in range(i, count)]


def block(index):
    return pl.ds(index * LANES, LANES)


def iotas(shape):
    return lax.broadcasted_iota(jnp.int32, shape, 0), lax.broadcasted_iota(jnp.int32, shape, 1)


def piece_rows(rows, devices):
    share = -(-rows // devices)
    return -(-share // 8) * 8


class Summer:
    def __init__(self, counts, rows):
        self.counts, self.used = counts, rows
        self.devices = counts[0] * counts[1]
        self.piece = piece_rows(rows, self.devices)
        self.owners = -(-rows // self.piece)
        self.rows = self.owners * self.piece

    def scratch(self):
        return [
            pltpu.VMEM((self.rows, LANES), jnp.float32),
            pltpu.VMEM((self.devices - 1, self.piece, LANES), jnp.float32),
            pltpu.VMEM((self.rows, LANES), jnp.float32),
            pltpu.SemaphoreType.DMA((4,)),
        ]

    def bind(self, me, part, inbox, total, sems):
        self.me, self.part, self.inbox, self.total, self.sems = me, part, inbox, total, sems
        return self

    def peer(self, offset):
        return lax.rem(self.me + offset, self.devices)

    def place(self, device):
        return (device // self.counts[1], lax.rem(device, self.counts[1]))

    def rows_of(self, device):
        return pl.ds(pl.multiple_of(device * self.piece, 8), self.piece)

    def is_owner(self, device, action):
        if self.owners == self.devices:
            action()
        else:
            pl.when(device < self.owners)(action)

    def greet(self):
        barrier = pltpu.get_barrier_semaphore()

        def signal(offset, carry):
            pl.semaphore_signal(
                barrier, inc=1, device_id=self.place(self.peer(offset)), device_id_type=pl.DeviceIdType.MESH
            )
            return carry

        lax.fori_loop(1, self.devices, signal, 0)

    def greeted(self):
        pl.semaphore_wait(pltpu.get_barrier_semaphore(), self.devices - 1)

    def outgoing(self, offset):
        peer = self.peer(offset)
        return pltpu.make_async_remote_copy(
            src_ref=self.part.at[self.rows_of(peer)],
            dst_ref=self.inbox.at[offset - 1],
            send_sem=self.sems.at[0],
            recv_sem=self.sems.at[1],
            device_id=self.place(peer),
            device_id_type=pl.DeviceIdType.MESH,
        )

    def spread(self, offset):
        mine = self.total.at[self.rows_of(self.me)]
        return pltpu.make_async_remote_copy(
            src_ref=mine,
            dst_ref=mine,
            send_sem=self.sems.at[2],
            recv_sem=self.sems.at[3],
            device_id=self.place(self.peer(offset)),
            device_id_type=pl.DeviceIdType.MESH,
        )

    def each_peer(self, action):
        def step(offset, carry):
            action(offset)
            return carry

        lax.fori_loop(1, self.devices, step, 0)

    def start(self):
        if self.rows > self.used:
            spare = self.rows - self.used
            self.part[pl.ds(self.used, spare), :] = jnp.zeros((spare, LANES), jnp.float32)
        self.each_peer(lambda offset: self.is_owner(self.peer(offset), lambda: self.outgoing(offset).start()))

    def reduce(self):
        def owned():
            pltpu.make_async_copy(self.inbox, self.inbox, self.sems.at[1]).wait()
            mine = self.rows_of(self.me)
            summed = self.part[mine, :]
            for slot in range(self.devices - 1):
                summed = summed + self.inbox[slot]
            self.total[mine, :] = summed
            self.each_peer(lambda offset: self.spread(offset).start())

        self.is_owner(self.me, owned)

    def wait_rows(self, rows):
        view = self.total.at[pl.ds(0, rows)]
        pltpu.make_async_copy(view, view, self.sems.at[3]).wait()

    def gathered(self):
        if self.owners == self.devices:
            self.wait_rows(self.rows - self.piece)
        else:
            pl.when(self.me < self.owners)(lambda: self.wait_rows(self.rows - self.piece))
            pl.when(self.me >= self.owners)(lambda: self.wait_rows(self.rows))

    def settle(self):
        self.each_peer(lambda offset: self.is_owner(self.peer(offset), lambda: self.outgoing(offset).wait_send()))
        self.is_owner(self.me, lambda: self.each_peer(lambda offset: self.spread(offset).wait_send()))


class Paired:
    def __init__(self, counts, rows):
        assert counts[1] == 2
        self.devices, self.used = counts[0], rows
        self.half = rows // 2
        self.piece = piece_rows(self.half, self.devices)
        self.owners = -(-self.half // self.piece)
        self.padded = self.owners * self.piece

    def scratch(self):
        return [
            pltpu.VMEM((2 * self.padded, LANES), jnp.float32),
            pltpu.VMEM((self.half, LANES), jnp.float32),
            pltpu.VMEM((self.devices - 1, self.piece, LANES), jnp.float32),
            pltpu.VMEM((2 * self.padded, LANES), jnp.float32),
            pltpu.SemaphoreType.DMA((8,)),
        ]

    def bind(self, row, core, part, box, inbox, total, sems):
        self.row, self.core, self.part, self.box, self.inbox, self.total, self.sems = (
            row, core, part, box, inbox, total, sems,
        )
        return self

    def spans(self, start, count):
        result, at = [], start
        while at < start + count:
            end = start + count if at >= self.half else min(self.half, start + count)
            place = at if at < self.half else self.padded + at - self.half
            result.append((place, at - start, end - at))
            at = end
        return result

    def put(self, index, value):
        for place, offset, rows in self.spans(index * LANES, LANES):
            self.part[pl.ds(place, rows), :] = value[offset : offset + rows, :]

    def get(self, index):
        pieces = [self.total[pl.ds(place, rows), :] for place, _, rows in self.spans(index * LANES, LANES)]
        return pieces[0] if len(pieces) == 1 else jnp.concatenate(pieces, axis=0)

    def half_of(self, core, rows):
        return pl.ds(pl.multiple_of(core * self.padded, 8), rows)

    def rows_of(self, device):
        return pl.ds(pl.multiple_of(self.core * self.padded + device * self.piece, 8), self.piece)

    def peer(self, offset):
        return lax.rem(self.row + offset, self.devices)

    def copy(self, source, target, sem, row, core):
        return pltpu.make_async_remote_copy(
            src_ref=source,
            dst_ref=target,
            send_sem=self.sems.at[sem],
            recv_sem=self.sems.at[sem + 1],
            device_id=(row, core),
            device_id_type=pl.DeviceIdType.MESH,
        )

    def pairing(self):
        return self.copy(self.part.at[self.half_of(1 - self.core, self.half)], self.box, 0, self.row, 1 - self.core)

    def outgoing(self, offset):
        return self.copy(
            self.part.at[self.rows_of(self.peer(offset))], self.inbox.at[offset - 1], 2, self.peer(offset), self.core
        )

    def spread(self, offset):
        mine = self.total.at[self.rows_of(self.row)]
        return self.copy(mine, mine, 4, self.peer(offset), self.core)

    def sharing(self):
        mine = self.total.at[self.half_of(self.core, self.padded)]
        return self.copy(mine, mine, 6, self.row, 1 - self.core)

    def each_peer(self, action):
        def step(offset, carry):
            action(offset)
            return carry

        lax.fori_loop(1, self.devices, step, 0)

    def is_owner(self, device, action):
        if self.owners == self.devices:
            action()
        else:
            pl.when(device < self.owners)(action)

    def pair_start(self):
        self.pairing().start()

    def pair_add(self):
        self.pairing().wait_recv()
        mine = self.half_of(self.core, self.half)
        self.part[mine, :] = self.part[mine, :] + self.box[...]
        if self.padded > self.half:
            spare = self.padded - self.half
            place = pl.ds(pl.multiple_of(self.core * self.padded + self.half, 8), spare)
            self.part[place, :] = jnp.zeros((spare, LANES), jnp.float32)

    def scatter(self):
        self.each_peer(lambda offset: self.is_owner(self.peer(offset), lambda: self.outgoing(offset).start()))

    def reduce(self):
        def owned():
            pltpu.make_async_copy(self.inbox, self.inbox, self.sems.at[3]).wait()
            mine = self.rows_of(self.row)
            summed = self.part[mine, :]
            for slot in range(self.devices - 1):
                summed = summed + self.inbox[slot]
            self.total[mine, :] = summed
            self.each_peer(lambda offset: self.spread(offset).start())

        self.is_owner(self.row, owned)

    def wait_rows(self, rows):
        view = self.total.at[pl.ds(0, rows)]
        pltpu.make_async_copy(view, view, self.sems.at[5]).wait()

    def share(self):
        if self.owners == self.devices:
            self.wait_rows(self.padded - self.piece)
        else:
            pl.when(self.row < self.owners)(lambda: self.wait_rows(self.padded - self.piece))
            pl.when(self.row >= self.owners)(lambda: self.wait_rows(self.padded))
        self.sharing().start()

    def shared(self):
        self.sharing().wait_recv()

    def settle(self):
        self.pairing().wait_send()
        self.each_peer(lambda offset: self.is_owner(self.peer(offset), lambda: self.outgoing(offset).wait_send()))
        self.is_owner(self.row, lambda: self.each_peer(lambda offset: self.spread(offset).wait_send()))
        self.sharing().wait_send()


def eliminate(pieces, first):
    sub, lane = iotas((SUBLANES, LANES))
    cols = [
        [jnp.broadcast_to(piece[0][:, first + k : first + k + 1], (SUBLANES, LANES)) for piece in pieces]
        for k in range(PANEL)
    ]
    roots = []
    for k in range(PANEL):
        own, at = k // SUBLANES, k % SUBLANES
        root = lax.rsqrt(cols[k][own][at : at + 1, :])
        roots.append(root)
        factors = {}
        for i in range(own, len(pieces)):
            factor = cols[k][i] * root
            if i > own:
                factors[i] = factor
            elif at < SUBLANES - 1:
                factors[i] = jnp.where(sub > at, factor, 0.0)
        for later in range(k + 1, PANEL):
            value = cols[later][own][at : at + 1, :] * root
            for i, factor in factors.items():
                cols[later][i] = cols[later][i] - factor * value
        for tile in range(2):
            row = pieces[own][tile][at : at + 1, :] * root
            for i, factor in factors.items():
                pieces[i][tile] = pieces[i][tile] - factor * row
    for own in range(PANEL // SUBLANES):
        scale = jnp.broadcast_to(roots[own * SUBLANES], (SUBLANES, LANES))
        for at in range(1, SUBLANES):
            scale = jnp.where(sub == at, roots[own * SUBLANES + at], scale)
        kept = lane >= first + own * SUBLANES + sub
        pieces[own][0] = jnp.where(kept, pieces[own][0] * scale, 0.0)
        pieces[own][1] = pieces[own][1] * scale


def factor_block(work):
    step, count = 2 * PANEL, PANEL // SUBLANES
    for top in range(0, LANES, step):
        pieces = []
        for row in range(top, top + step, SUBLANES):
            pieces.append([work[row : row + SUBLANES, 0:LANES], work[row : row + SUBLANES, LANES : 2 * LANES]])
        eliminate(pieces, top)
        done, pieces = pieces[:count], pieces[count:]
        eliminate(pieces, top + PANEL)
        done = done + pieces
        left = jnp.concatenate([piece[0] for piece in done], axis=0)
        right = jnp.concatenate([piece[1] for piece in done], axis=0)
        both = jnp.concatenate([left, right], axis=1)
        work[top : top + step, :] = both
        below = top + step
        if below < LANES:
            work[below:, :] = work[below:, :] - dot6(left, both, TN)[below:, :]


def upto(count):
    return pl.ds(0, count * LANES)


def factor_column(b, column, shift, work, upper, inverse):
    row, lane = iotas((LANES, LANES))
    eye = jnp.where(row == lane, 1.0, 0.0).astype(jnp.float32)
    diagonal = column[b] + shift * eye
    carried = None
    if b:
        above = jnp.concatenate(column[:b], axis=0)
        above = dot6(inverse[upto(b), upto(b)], above)
        upper[upto(b), block(b)] = above
        diagonal = diagonal - dot6(above, above, TN)
        carried = dot6(above, inverse[upto(b), upto(b)], TN)
    work[:, pl.ds(0, LANES)] = diagonal
    work[:, pl.ds(LANES, LANES)] = eye
    factor_block(work)
    upper[block(b), block(b)] = work[:, pl.ds(0, LANES)]
    inv = work[:, pl.ds(LANES, LANES)]
    inverse[block(b), block(b)] = inv
    zero = jnp.zeros((LANES, LANES), jnp.float32)
    for j in range(b):
        upper[block(b), block(j)] = zero
        inverse[block(j), block(b)] = zero
    if b:
        inverse[block(b), upto(b)] = -dot6(inv, carried)


def upper_times_lower(width, left, right, dot=dot3):
    columns = []
    for j in range(width):
        at = j * LANES
        columns.append(dot(left[0 : at + LANES, at:], right[at:, at : at + LANES]))
    return columns


def lower_times_upper(width, left, right, dot=dot3):
    rows = []
    for i in range(width):
        at = i * LANES
        rows.append(dot(left[at : at + LANES, 0 : at + LANES], right[0 : at + LANES, at:]))
    return rows


def from_columns(width, columns):
    size = width * LANES
    full = []
    for j, column in enumerate(columns):
        spare = size - column.shape[0]
        full.append(jnp.concatenate([column, jnp.zeros((spare, LANES), jnp.float32)], axis=0) if spare else column)
    return jnp.concatenate(full, axis=1)


def from_rows(width, rows):
    size = width * LANES
    full = []
    for row in rows:
        spare = size - row.shape[1]
        full.append(jnp.concatenate([jnp.zeros((LANES, spare), jnp.float32), row], axis=1) if spare else row)
    return jnp.concatenate(full, axis=0)


def symmetric_half(width, grad, upper):
    row, lane = iotas(grad.shape)
    kept = jnp.where(row <= lane, grad, 0.0)
    columns = []
    for j in range(width):
        at = j * LANES
        columns.append(dot3(kept[0 : at + LANES, at:], upper[at : at + LANES, at:], NT))
    product = from_columns(width, columns)
    phi = jnp.where(row < lane, product, jnp.where(row == lane, 0.5 * product, 0.0))
    return 0.5 * (phi + phi.T), phi


def whole_kernel(counts, width, matrix, q_grad, grad_factor, out, *scratch):
    scratch = list(scratch)

    def take(count):
        taken = scratch[:count]
        del scratch[:count]
        return taken

    row, core = lax.axis_index("rows"), lax.axis_index("sub")
    me = row * counts[1] + core
    size = width * LANES
    rate = shift_frac / size
    pairs = [(i, b) for b in range(width) for i in range(b + 1)]
    head, rest, later, cross = summers(counts, width)
    head.bind(me, *take(4))
    rest.bind(row, core, *take(5))
    for summer in later:
        summer.bind(me, *take(4))
    cross.bind(row, core, *take(5))
    work, upper1, inverse1, upper2, inverse2, current, held, early = scratch

    head.greet()
    head.part[block(0), :] = dot6(matrix[:, block(0)], matrix[:, block(0)], TN)
    squares = jnp.sum(matrix[...] * matrix[...])
    head.part[pl.ds(LANES, SUBLANES), :] = jnp.full((SUBLANES, LANES), squares, jnp.float32)
    for index, (i, j) in enumerate(pairs[1:]):
        rest.put(index, dot6(matrix[:, block(i)], matrix[:, block(j)], TN))
    for index, (i, j) in enumerate(pairs):
        cross.put(index, dot6(matrix[:, block(i)], q_grad[:, block(j)], TN))
    head.greeted()
    head.start()
    rest.pair_start()
    cross.pair_start()
    rest.pair_add()
    rest.scatter()
    cross.pair_add()
    head.reduce()
    rest.reduce()
    cross.scatter()
    head.gathered()
    shift1 = rate * head.total[pl.ds(LANES, SUBLANES), :][0:1, :]

    def section1(b):
        if b == 0:
            column = [head.total[block(0), :]]
        else:
            column = [rest.get(pairs.index((i, b)) - 1) for i in range(b + 1)]
        factor_column(b, column, shift1, work, upper1, inverse1)
        current[:, block(b)] = dot6(matrix[:, upto(b + 1)], inverse1[block(b), upto(b + 1)], NT)
        later[b].part[upto(b + 1), :] = dot6(current[:, upto(b + 1)], current[:, block(b)], TN)
        later[b].start()

    for b in range(width):
        section1(b)
        if b == 0:
            rest.share()
            cross.reduce()
            rest.shared()
        if b == 1:
            later[0].reduce()
            cross.share()
    inverse = inverse1[...]
    squares = jnp.sum(inverse * inverse)
    shift2 = rate * (size - shift1 * squares)
    for summer in later[1:-1]:
        summer.reduce()
    cross.shared()
    crossed = [[cross.get(pairs.index((i, j))) if i <= j else None for j in range(width)] for i in range(width)]
    crossed = from_rows(width, [jnp.concatenate(crossed[i][i:], axis=1) for i in range(width)])
    held[...] = from_rows(width, lower_times_upper(width, inverse1, crossed, dot6))
    early[...] = dot3(grad_factor[...], upper1[...], NT)
    for b in range(width):
        if b == 1 or width == 1:
            later[-1].reduce()
        later[b].gathered()
        column = [later[b].total[block(i), :] for i in range(b + 1)]
        factor_column(b, column, shift2, work, upper2, inverse2)

    row, lane = iotas((size, size))
    inverse = inverse2[...]
    turned = from_columns(width, upper_times_lower(width, held[...], inverse))
    total2 = early[...] - from_rows(width, lower_times_upper(width, inverse, turned))
    half2, _ = symmetric_half(width, total2, upper2)
    middle = dot3(half2, inverse)
    trace2 = rate * jnp.sum(middle * inverse)
    gram = from_columns(width, [summer.total[upto(b + 1), :] for b, summer in enumerate(later)])
    wide2 = jnp.concatenate([shift2] * width, axis=1)
    across = dot3(upper2[...] - wide2 * inverse, middle, TN)
    crossed1 = turned + 2.0 * (across + trace2 * gram)
    total1 = dot3(upper2[...], grad_factor[...], TN) - from_columns(
        width, upper_times_lower(width, crossed1, inverse1)
    )
    half1, phi1 = symmetric_half(width, total1, upper1)
    missing = jnp.where(row == lane, 1.0 - gram, -gram)
    trace1 = rate * jnp.sum(phi1 * missing) / shift1
    after = dot3(current[...], inverse, NT)
    grad = dot3(q_grad[...], inverse) + 2.0 * (dot3(after, middle) + trace2 * current[...])
    grad = grad + 2.0 * dot3(current[...], half1)
    wide1 = jnp.concatenate([trace1] * width, axis=1)
    out[...] = dot3(grad, inverse1[...]) + 2.0 * wide1 * matrix[...]
    for summer in [head, rest, *later, cross]:
        summer.settle()


def summers(counts, width):
    count = width * (width + 1) // 2
    later = [Summer(counts, (b + 1) * LANES) for b in range(width)]
    return Summer(counts, LANES + SUBLANES), Paired(counts, (count - 1) * LANES), later, Paired(counts, count * LANES)


def per_device(counts, matrix, grad_out, grad_factor):
    rows, size = matrix.shape
    width = size // LANES
    vmem = pl.BlockSpec(memory_space=pltpu.VMEM)
    square = pltpu.VMEM((size, size), jnp.float32)
    tall = pltpu.VMEM((rows, size), jnp.float32)
    work = pltpu.VMEM((LANES, 2 * LANES), jnp.float32)
    head, rest, later, cross = summers(counts, width)
    sums = []
    for summer in [head, rest, *later, cross]:
        sums = sums + summer.scratch()
    return pl.pallas_call(
        functools.partial(whole_kernel, counts, width),
        out_shape=jax.ShapeDtypeStruct((rows, size), jnp.float32),
        in_specs=[vmem] * 3,
        out_specs=vmem,
        scratch_shapes=sums + [work] + [square] * 4 + [tall, square, square],
        compiler_params=pltpu.CompilerParams(
            vmem_limit_bytes=VMEM_LIMIT, collective_id=0, has_side_effects=True
        ),
    )(matrix, grad_out, grad_factor)


def solution(mesh):
    counts = (mesh.shape["rows"], mesh.shape["sub"])
    placed = (P(("rows", "sub"), None), P(("rows", "sub"), None), P())
    return jax.shard_map(
        functools.partial(per_device, counts),
        mesh=mesh,
        in_specs=placed,
        out_specs=P(("rows", "sub"), None),
        check_vma=False,
    )
```

time: 101 us -> 68.6 us (0.68)
  the two profiles are of different devices: /device:TPU:29 before, /device:TPU:0 now
where the time goes in v2:
time: 68.6 us; the launch traced here: 68.5 us
  Pallas kernels  66.9 us (98%)
  local copies, waits for them, and re-layouts  1.62 us (2%)
    pallas_call x1, Pallas kernels, per_device(): pl.pallas_call(functools.partial(whole_kernel, counts, width), out_shape=...  66.9 us
    unnamed x1, local copies, waits for them, and re-layouts  1.62 us

profile of v2, /device:TPU:0, one launch (start us, length us, event | category | flops | bytes accessed | tf_op | source)
XLA Modules:
  0.0 68.5 jit_solution(9150443024759513548)
XLA Ops:
  0.0 66.9 %shard_map.37 = f32[128,384]{1,0:T(8,128)} custom-call(f32[128,384]{1,0:T(8,128)} %matrix.1, f32[128,384]{1,0:T(8,128)} %q_grad.1, f32[384,384]{1,0:T(8,128)} %grad_factor.1), custom_call_target="tpu_custom_call" | custom-call | tf_op jit(solution)/shard_map/pallas_call | solution.py:565
  66.9 1.6 %copy.5 = f32[128,384]{1,0:T(8,128)} copy(f32[128,384]{1,0:T(8,128)} %shard_map.37) | data formatting | bytes 393216

commit v3 on v2

v3 whole, which is shorter than its diff:
```python
import functools

import jax
import jax.numpy as jnp
from jax import lax
from jax.experimental import pallas as pl
from jax.experimental.pallas import tpu as pltpu
from jax.sharding import PartitionSpec as P

LANES = 128
PANEL = 16
GROUP = 5
SUBLANES = 8
shift_frac = 0.02
VMEM_LIMIT = 56 * 1024 * 1024


NN, NT, TN = ((1,), (0,)), ((1,), (1,)), ((0,), (0,))


def halves(value):
    high = value.astype(jnp.bfloat16)
    return high, (value - high.astype(jnp.float32)).astype(jnp.bfloat16)


def thirds(value):
    high = value.astype(jnp.bfloat16)
    rest = value - high.astype(jnp.float32)
    middle = rest.astype(jnp.bfloat16)
    return high, middle, (rest - middle.astype(jnp.float32)).astype(jnp.bfloat16)


def joined(left, right, dims):
    (left_axis,), (right_axis,) = dims
    left, right = jnp.concatenate(left, axis=left_axis), jnp.concatenate(right, axis=right_axis)
    return lax.dot_general(left, right, (dims, ((), ())), preferred_element_type=jnp.float32)


def dot6(left, right, dims=NN):
    (a, b, c), (d, e, f) = thirds(left), thirds(right)
    return joined([a, a, b, a, c, b], [d, e, d, f, d, e], dims)


def dot3(left, right, dims=NN):
    (a, b), (d, e) = halves(left), halves(right)
    return joined([a, a, b], [d, e, d], dims)


def upper_pairs(count):
    return [(i, j) for i in range(count) for j in range(i, count)]


def block(index):
    return pl.ds(index * LANES, LANES)


def iotas(shape):
    return lax.broadcasted_iota(jnp.int32, shape, 0), lax.broadcasted_iota(jnp.int32, shape, 1)


def piece_rows(rows, devices):
    share = -(-rows // devices)
    return -(-share // 8) * 8


def each_row(count, action):
    whole, left = divmod(count - 1, GROUP)

    def trip(index, carry):
        for k in range(GROUP):
            action(index * GROUP + (k + 1))
        return carry

    lax.fori_loop(0, whole, trip, 0)
    for k in range(left):
        action(whole * GROUP + k + 1)


def bytes_of(view, sem):
    pltpu.make_async_copy(view, view, sem).wait()


def greet(counts, row, core):
    barrier = pltpu.get_barrier_semaphore()

    def signal(target, place):
        pl.semaphore_signal(barrier, inc=1, device_id=(target, place), device_id_type=pl.DeviceIdType.MESH)

    def both(offset):
        peer = lax.rem(row + offset, counts[0])
        for place in range(counts[1]):
            signal(peer, place)

    each_row(counts[0], both)
    signal(row, 1 - core)


def greeted(counts):
    pl.semaphore_wait(pltpu.get_barrier_semaphore(), counts[0] * counts[1] - 1)


class Direct:
    def __init__(self, counts, rows):
        assert counts[1] == 2
        self.devices, self.used = counts[0], rows
        self.piece = piece_rows(rows, self.devices)
        self.owners = -(-rows // self.piece)

    def scratch(self):
        return [
            pltpu.VMEM((self.owners * self.piece, LANES), jnp.float32),
            pltpu.VMEM((2 * self.devices - 1, self.piece, LANES), jnp.float32),
            pltpu.VMEM((self.owners * self.piece, LANES), jnp.float32),
            pltpu.SemaphoreType.DMA((4,)),
        ]

    def bind(self, row, core, part, inbox, total, sems):
        self.row, self.core, self.part, self.inbox, self.total, self.sems = row, core, part, inbox, total, sems
        return self

    def put(self, value):
        self.part[pl.ds(0, self.used), :] = value
        spare = self.owners * self.piece - self.used
        if spare:
            self.part[pl.ds(self.used, spare), :] = jnp.zeros((spare, LANES), jnp.float32)

    def get(self, start, count):
        return self.total[pl.ds(start, count), :]

    def peer(self, offset):
        return lax.rem(self.row + offset, self.devices)

    def rows_of(self, device):
        return pl.ds(pl.multiple_of(device * self.piece, 8), self.piece)

    def is_owner(self, row, action):
        if self.owners == self.devices:
            action()
        else:
            pl.when(row < self.owners)(action)

    def copy(self, source, target, sem, row, core):
        return pltpu.make_async_remote_copy(
            src_ref=source,
            dst_ref=target,
            send_sem=self.sems.at[sem],
            recv_sem=self.sems.at[sem + 1],
            device_id=(row, core),
            device_id_type=pl.DeviceIdType.MESH,
        )

    def outgoing(self, row, slot):
        return self.copy(self.part.at[self.rows_of(row)], self.inbox.at[slot], 0, row, 1)

    def spread(self, row, core):
        mine = self.total.at[self.rows_of(self.row)]
        return self.copy(mine, mine, 2, row, core)

    def start(self):
        def send(offset):
            peer = self.peer(offset)
            self.is_owner(peer, lambda: self.outgoing(peer, 2 * offset + self.core - 1).start())

        pl.when(self.core == 0)(lambda: self.is_owner(self.row, lambda: self.outgoing(self.row, 0).start()))
        each_row(self.devices, send)

    def owned(self, action):
        pl.when(self.core == 1)(lambda: self.is_owner(self.row, action))

    def reduce(self):
        def summed():
            bytes_of(self.inbox, self.sems.at[1])
            mine = self.rows_of(self.row)
            terms = [self.part[mine, :]] + [self.inbox[slot] for slot in range(2 * self.devices - 1)]
            while len(terms) > 1:
                odd = terms[len(terms) // 2 * 2 :]
                terms = [terms[k] + terms[k + 1] for k in range(0, len(terms) - 1, 2)] + odd
            self.total[mine, :] = terms[0]

            def send(offset):
                for core in (1, 0):
                    self.spread(self.peer(offset), core).start()

            each_row(self.devices, send)
            self.spread(self.row, 0).start()

        self.owned(summed)

    def gathered(self):
        rows = self.owners * self.piece
        full = self.total.at[pl.ds(0, rows)]
        if self.owners == self.devices:
            pl.when(self.core == 0)(lambda: bytes_of(full, self.sems.at[3]))
            others = self.total.at[pl.ds(0, rows - self.piece)]
            pl.when(self.core == 1)(lambda: bytes_of(others, self.sems.at[3]))
            return
        mine = (self.core == 1) & (self.row < self.owners)
        if self.owners > 1:
            others = self.total.at[pl.ds(0, rows - self.piece)]
            pl.when(mine)(lambda: bytes_of(others, self.sems.at[3]))
        pl.when(jnp.logical_not(mine))(lambda: bytes_of(full, self.sems.at[3]))

    def settle(self):
        rows = self.owners * self.piece
        full = self.part.at[pl.ds(0, rows)]
        if self.owners == self.devices:
            pl.when(self.core == 0)(lambda: bytes_of(full, self.sems.at[0]))
            others = self.part.at[pl.ds(0, rows - self.piece)]
            pl.when(self.core == 1)(lambda: bytes_of(others, self.sems.at[0]))
        else:
            mine = self.row < self.owners
            keeps = (self.core == 1) & mine
            if self.owners > 1:
                others = self.part.at[pl.ds(0, rows - self.piece)]
                pl.when(keeps)(lambda: bytes_of(others, self.sems.at[0]))
            pl.when(jnp.logical_not(keeps))(lambda: bytes_of(full, self.sems.at[0]))
        self.owned(lambda: bytes_of(self.inbox, self.sems.at[2]))


class Paired:
    def __init__(self, counts, rows):
        assert counts[1] == 2
        self.devices, self.used = counts[0], rows
        self.half = rows // 2
        self.piece = piece_rows(self.half, self.devices)
        self.owners = -(-self.half // self.piece)
        self.padded = self.owners * self.piece

    def scratch(self):
        return [
            pltpu.VMEM((2 * self.padded, LANES), jnp.float32),
            pltpu.VMEM((self.half, LANES), jnp.float32),
            pltpu.VMEM((self.devices - 1, self.piece, LANES), jnp.float32),
            pltpu.VMEM((2 * self.padded, LANES), jnp.float32),
            pltpu.SemaphoreType.DMA((8,)),
        ]

    def bind(self, row, core, part, box, inbox, total, sems):
        self.row, self.core, self.part, self.box, self.inbox, self.total, self.sems = (
            row, core, part, box, inbox, total, sems,
        )
        return self

    def spans(self, start, count):
        result, at = [], start
        while at < start + count:
            end = start + count if at >= self.half else min(self.half, start + count)
            place = at if at < self.half else self.padded + at - self.half
            result.append((place, at - start, end - at))
            at = end
        return result

    def put(self, index, value):
        for place, offset, rows in self.spans(index * LANES, LANES):
            self.part[pl.ds(place, rows), :] = value[offset : offset + rows, :]

    def get(self, index):
        pieces = [self.total[pl.ds(place, rows), :] for place, _, rows in self.spans(index * LANES, LANES)]
        return pieces[0] if len(pieces) == 1 else jnp.concatenate(pieces, axis=0)

    def half_of(self, core, rows):
        return pl.ds(pl.multiple_of(core * self.padded, 8), rows)

    def rows_of(self, device):
        return pl.ds(pl.multiple_of(self.core * self.padded + device * self.piece, 8), self.piece)

    def peer(self, offset):
        return lax.rem(self.row + offset, self.devices)

    def copy(self, source, target, sem, row, core):
        return pltpu.make_async_remote_copy(
            src_ref=source,
            dst_ref=target,
            send_sem=self.sems.at[sem],
            recv_sem=self.sems.at[sem + 1],
            device_id=(row, core),
            device_id_type=pl.DeviceIdType.MESH,
        )

    def pairing(self):
        return self.copy(self.part.at[self.half_of(1 - self.core, self.half)], self.box, 0, self.row, 1 - self.core)

    def outgoing(self, offset):
        return self.copy(
            self.part.at[self.rows_of(self.peer(offset))], self.inbox.at[offset - 1], 2, self.peer(offset), self.core
        )

    def spread(self, offset):
        mine = self.total.at[self.rows_of(self.row)]
        return self.copy(mine, mine, 4, self.peer(offset), self.core)

    def sharing(self):
        mine = self.total.at[self.half_of(self.core, self.padded)]
        return self.copy(mine, mine, 6, self.row, 1 - self.core)

    def is_owner(self, device, action):
        if self.owners == self.devices:
            action()
        else:
            pl.when(device < self.owners)(action)

    def pair_start(self):
        self.pairing().start()

    def pair_add(self):
        self.pairing().wait_recv()
        mine = self.half_of(self.core, self.half)
        self.part[mine, :] = self.part[mine, :] + self.box[...]
        if self.padded > self.half:
            spare = self.padded - self.half
            place = pl.ds(pl.multiple_of(self.core * self.padded + self.half, 8), spare)
            self.part[place, :] = jnp.zeros((spare, LANES), jnp.float32)

    def scatter(self):
        each_row(self.devices, lambda offset: self.is_owner(self.peer(offset), lambda: self.outgoing(offset).start()))

    def reduce(self):
        def owned():
            bytes_of(self.inbox, self.sems.at[3])
            mine = self.rows_of(self.row)
            summed = self.part[mine, :]
            for slot in range(self.devices - 1):
                summed = summed + self.inbox[slot]
            self.total[mine, :] = summed
            each_row(self.devices, lambda offset: self.spread(offset).start())

        self.is_owner(self.row, owned)

    def wait_rows(self, rows):
        view = self.total.at[pl.ds(0, rows)]
        pltpu.make_async_copy(view, view, self.sems.at[5]).wait()

    def share(self):
        if self.owners == self.devices:
            self.wait_rows(self.padded - self.piece)
        else:
            pl.when(self.row < self.owners)(lambda: self.wait_rows(self.padded - self.piece))
            pl.when(self.row >= self.owners)(lambda: self.wait_rows(self.padded))
        self.sharing().start()

    def shared(self):
        self.sharing().wait_recv()

    def settle(self):
        self.pairing().wait_send()
        if self.owners == self.devices:
            bytes_of(self.inbox, self.sems.at[2])
        else:
            rows = self.padded - self.piece
            if rows:
                pl.when(self.row < self.owners)(lambda: bytes_of(self.part.at[pl.ds(0, rows)], self.sems.at[2]))
            full = self.part.at[pl.ds(0, self.padded)]
            pl.when(self.row >= self.owners)(lambda: bytes_of(full, self.sems.at[2]))
        self.is_owner(self.row, lambda: bytes_of(self.inbox, self.sems.at[4]))
        self.sharing().wait_send()


def eliminate(pieces, first):
    sub, lane = iotas((SUBLANES, LANES))
    cols = [
        [jnp.broadcast_to(piece[0][:, first + k : first + k + 1], (SUBLANES, LANES)) for piece in pieces]
        for k in range(PANEL)
    ]
    roots = []
    for k in range(PANEL):
        own, at = k // SUBLANES, k % SUBLANES
        root = lax.rsqrt(cols[k][own][at : at + 1, :])
        roots.append(root)
        factors = {}
        for i in range(own, len(pieces)):
            factor = cols[k][i] * root
            if i > own:
                factors[i] = factor
            elif at < SUBLANES - 1:
                factors[i] = jnp.where(sub > at, factor, 0.0)
        for later in range(k + 1, PANEL):
            value = cols[later][own][at : at + 1, :] * root
            for i, factor in factors.items():
                cols[later][i] = cols[later][i] - factor * value
        for tile in range(2):
            row = pieces[own][tile][at : at + 1, :] * root
            for i, factor in factors.items():
                pieces[i][tile] = pieces[i][tile] - factor * row
    for own in range(PANEL // SUBLANES):
        scale = jnp.broadcast_to(roots[own * SUBLANES], (SUBLANES, LANES))
        for at in range(1, SUBLANES):
            scale = jnp.where(sub == at, roots[own * SUBLANES + at], scale)
        kept = lane >= first + own * SUBLANES + sub
        pieces[own][0] = jnp.where(kept, pieces[own][0] * scale, 0.0)
        pieces[own][1] = pieces[own][1] * scale


def factor_block(work, hooks):
    step, count = 2 * PANEL, PANEL // SUBLANES
    for top in range(0, LANES, step):
        hooks.get(top // step, lambda: None)()
        pieces = []
        for row in range(top, top + step, SUBLANES):
            pieces.append([work[row : row + SUBLANES, 0:LANES], work[row : row + SUBLANES, LANES : 2 * LANES]])
        eliminate(pieces, top)
        done, pieces = pieces[:count], pieces[count:]
        eliminate(pieces, top + PANEL)
        done = done + pieces
        left = jnp.concatenate([piece[0] for piece in done], axis=0)
        right = jnp.concatenate([piece[1] for piece in done], axis=0)
        both = jnp.concatenate([left, right], axis=1)
        work[top : top + step, :] = both
        below = top + step
        if below < LANES:
            work[below:, :] = work[below:, :] - dot6(left, both, TN)[below:, :]


def upto(count):
    return pl.ds(0, count * LANES)


def prepare(b, above, upper, inverse):
    above = dot6(inverse[upto(b), upto(b)], above)
    upper[upto(b), block(b)] = above
    return dot6(above, above, TN), dot6(above, inverse[upto(b), upto(b)], TN)


def factor_column(b, diagonal, prepared, shift, work, upper, inverse, hooks):
    row, lane = iotas((LANES, LANES))
    eye = jnp.where(row == lane, 1.0, 0.0).astype(jnp.float32)
    diagonal = diagonal + shift * eye
    work[:, pl.ds(0, LANES)] = diagonal - prepared[0] if b else diagonal
    work[:, pl.ds(LANES, LANES)] = eye
    factor_block(work, hooks)
    upper[block(b), block(b)] = work[:, pl.ds(0, LANES)]
    inv = work[:, pl.ds(LANES, LANES)]
    inverse[block(b), block(b)] = inv
    zero = jnp.zeros((LANES, LANES), jnp.float32)
    for j in range(b):
        upper[block(b), block(j)] = zero
        inverse[block(j), block(b)] = zero
    if b:
        inverse[block(b), upto(b)] = -dot6(inv, prepared[1])


def upper_times_lower(width, left, right, dot=dot3):
    columns = []
    for j in range(width):
        at = j * LANES
        columns.append(dot(left[0 : at + LANES, at:], right[at:, at : at + LANES]))
    return columns


def lower_times_upper(width, left, right, dot=dot3):
    rows = []
    for i in range(width):
        at = i * LANES
        rows.append(dot(left[at : at + LANES, 0 : at + LANES], right[0 : at + LANES, at:]))
    return rows


def from_columns(width, columns):
    size = width * LANES
    full = []
    for j, column in enumerate(columns):
        spare = size - column.shape[0]
        full.append(jnp.concatenate([column, jnp.zeros((spare, LANES), jnp.float32)], axis=0) if spare else column)
    return jnp.concatenate(full, axis=1)


def from_rows(width, rows):
    size = width * LANES
    full = []
    for row in rows:
        spare = size - row.shape[1]
        full.append(jnp.concatenate([jnp.zeros((LANES, spare), jnp.float32), row], axis=1) if spare else row)
    return jnp.concatenate(full, axis=0)


def symmetric_half(width, grad, upper):
    row, lane = iotas(grad.shape)
    kept = jnp.where(row <= lane, grad, 0.0)
    columns = []
    for j in range(width):
        at = j * LANES
        columns.append(dot3(kept[0 : at + LANES, at:], upper[at : at + LANES, at:], NT))
    product = from_columns(width, columns)
    phi = jnp.where(row < lane, product, jnp.where(row == lane, 0.5 * product, 0.0))
    return 0.5 * (phi + phi.T), phi


def whole_kernel(counts, width, matrix_in, q_grad_in, grad_factor_in, out, *scratch):
    scratch = list(scratch)

    def take(count):
        taken = scratch[:count]
        del scratch[:count]
        return taken

    row, core = lax.axis_index("rows"), lax.axis_index("sub")
    size = width * LANES
    rate = shift_frac / size
    last = width - 1
    pairs = [(i, b) for b in range(width) for i in range(b + 1)]
    all_sums = summers(counts, width)
    head, rest, later, off, cross = all_sums
    for summer in flat(all_sums):
        summer.bind(row, core, *take(len(summer.scratch())))
    matrix, q_grad, grad_factor, loads, work, upper1, inverse1, upper2, inverse2, current, held, early = scratch

    loading = []
    for index, (source, target) in enumerate(
        [(matrix_in, matrix), (q_grad_in, q_grad), (grad_factor_in, grad_factor)]
    ):
        loading.append(pltpu.make_async_copy(source, target, loads.at[index]))
        loading[-1].start()
    greet(counts, row, core)
    loading[0].wait()
    squares = jnp.sum(matrix[...] * matrix[...])
    line, lane = iotas((LANES, LANES))
    corner = (line == LANES - 1) & (lane == 0)
    head.put(jnp.where(corner, squares, dot6(matrix[:, block(0)], matrix[:, block(0)], TN)))
    for b in range(1, width):
        for i in range(b + 1):
            rest[b - 1].put(i, dot6(matrix[:, block(i)], matrix[:, block(b)], TN))
    loading[1].wait()
    for index, (i, j) in enumerate(pairs):
        cross.put(index, dot6(matrix[:, block(i)], q_grad[:, block(j)], TN))
    loading[2].wait()
    greeted(counts)
    head.start()
    for summer in rest + [cross]:
        summer.pair_start()
    for summer in rest:
        summer.pair_add()
        summer.scatter()
    cross.pair_add()
    head.reduce()
    for summer in rest:
        summer.reduce()
    cross.scatter()
    head.gathered()
    first_block = head.get(0, LANES)
    shift1 = rate * jnp.broadcast_to(first_block[LANES - 1 : LANES, 0:1], (1, LANES))
    first_block = jnp.where(corner, first_block[0:1, LANES - 1 : LANES], first_block)

    def rest_share():
        for summer in rest[1:]:
            summer.share()

    def off_on():
        later[0].reduce()
        off.pair_add()
        off.scatter()

    hooks1 = {0: {2: lambda: rest[0].share()}, 1: {1: rest_share}, last: {1: off_on, 3: cross.share}}
    for b in range(width):
        if b == 0:
            diagonal, prepared = first_block, None
        else:
            rest[b - 1].shared()
            above = jnp.concatenate([rest[b - 1].get(i) for i in range(b)], axis=0)
            diagonal, prepared = rest[b - 1].get(b), prepare(b, above, upper1, inverse1)
        if b == last:
            ahead = matrix[:, block(b)] - dot6(matrix[:, upto(b)], prepared[1], NT)
            for i in range(b):
                off.put(i, dot6(current[:, block(i)], ahead, TN))
            off.pair_start()
        factor_column(b, diagonal, prepared, shift1, work, upper1, inverse1, hooks1.get(b, {}))
        current[:, block(b)] = dot6(matrix[:, upto(b + 1)], inverse1[block(b), upto(b + 1)], NT)
        first = b if b == last else 0
        later[b].put(dot6(current[:, first * LANES : (b + 1) * LANES], current[:, block(b)], TN))
        later[b].start()
        if b == 0:
            cross.reduce()
    for summer in later[1:-1]:
        summer.reduce()
    inverse = inverse1[...]
    shift2 = rate * (size - shift1 * jnp.sum(inverse * inverse))
    columns = []
    for j in range(width):
        at = j * LANES
        columns.append(dot3(grad_factor[0 : at + LANES, at:], upper1[at : at + LANES, at:], NT))
    early[...] = from_columns(width, columns)
    hooks2 = {0: {1: off.reduce}, 1: {2: off.share}}
    gram = []
    for b in range(width):
        if b == last:
            off.shared()
            above = jnp.concatenate([off.get(i) for i in range(b)], axis=0)
            above = dot6(above, inverse1[block(b), block(b)], NT)
            prepared = prepare(b, above, upper2, inverse2)
            later[b].gathered()
            diagonal = later[b].get(0, LANES)
            gram.append(jnp.concatenate([above, diagonal], axis=0))
        else:
            later[b].gathered()
            gram.append(later[b].get(0, (b + 1) * LANES))
            diagonal = gram[b][b * LANES :, :]
            prepared = prepare(b, gram[b][: b * LANES, :], upper2, inverse2) if b else None
        factor_column(b, diagonal, prepared, shift2, work, upper2, inverse2, hooks2.get(b, {}))
        if b == 0:
            later[-1].reduce()
            cross.shared()
            crossed = [
                jnp.concatenate([cross.get(pairs.index((i, j))) for j in range(i, width)], axis=1)
                for i in range(width)
            ]
            held[...] = from_rows(
                width, lower_times_upper(width, inverse1, from_rows(width, crossed), dot6)
            )

    row, lane = iotas((size, size))
    inverse = inverse2[...]
    turned = from_columns(width, upper_times_lower(width, held[...], inverse))
    total2 = early[...] - from_rows(width, lower_times_upper(width, inverse, turned))
    half2, _ = symmetric_half(width, total2, upper2)
    middle = jnp.concatenate(
        [dot3(half2[:, j * LANES :], inverse[j * LANES :, j * LANES : (j + 1) * LANES]) for j in range(width)], axis=1
    )
    trace2 = rate * jnp.sum(middle * inverse)
    gram = from_columns(width, gram)
    wide2 = jnp.concatenate([shift2] * width, axis=1)
    mixed = upper2[...] - wide2 * inverse
    across = from_columns(
        width,
        [
            dot3(mixed[:, 0 : (j + 1) * LANES], middle[:, j * LANES : (j + 1) * LANES], TN)
            for j in range(width)
        ],
    )
    crossed1 = turned + 2.0 * (across + trace2 * gram)
    moved = []
    for i in range(width):
        at = i * LANES
        moved.append(dot3(upper2[0 : at + LANES, at : at + LANES], grad_factor[0 : at + LANES, at:], TN))
    total1 = from_rows(width, moved) - from_columns(width, upper_times_lower(width, crossed1, inverse1))
    half1, phi1 = symmetric_half(width, total1, upper1)
    missing = jnp.where(row == lane, 1.0 - gram, -gram)
    trace1 = rate * jnp.sum(phi1 * missing) / shift1
    after = dot3(current[...], inverse, NT)
    grad = dot3(q_grad[...], inverse) + 2.0 * (dot3(after, middle) + trace2 * current[...])
    grad = grad + 2.0 * dot3(current[...], half1)
    wide1 = jnp.concatenate([trace1] * width, axis=1)
    out[...] = dot3(grad, inverse1[...]) + 2.0 * wide1 * matrix[...]
    for summer in flat(all_sums):
        summer.settle()


def summers(counts, width):
    count = width * (width + 1) // 2
    rest = [Paired(counts, (b + 1) * LANES) for b in range(1, width)]
    later = [Direct(counts, (b + 1) * LANES) for b in range(width - 1)] + [Direct(counts, LANES)]
    off = Paired(counts, (width - 1) * LANES)
    return Direct(counts, LANES), rest, later, off, Paired(counts, count * LANES)


def flat(sums):
    head, rest, later, off, cross = sums
    return [head, *rest, *later, off, cross]


def per_device(counts, matrix, grad_out, grad_factor):
    rows, size = matrix.shape
    width = size // LANES
    vmem = pl.BlockSpec(memory_space=pltpu.VMEM)
    square = pltpu.VMEM((size, size), jnp.float32)
    tall = pltpu.VMEM((rows, size), jnp.float32)
    work = pltpu.VMEM((LANES, 2 * LANES), jnp.float32)
    sums = []
    for summer in flat(summers(counts, width)):
        sums = sums + summer.scratch()
    held = [tall, tall, square, pltpu.SemaphoreType.DMA((3,)), work] + [square] * 4 + [tall, square, square]
    return pl.pallas_call(
        functools.partial(whole_kernel, counts, width),
        out_shape=jax.ShapeDtypeStruct((rows, size), jnp.float32),
        in_specs=[pl.BlockSpec(memory_space=pl.ANY)] * 3,
        out_specs=vmem,
        scratch_shapes=sums + held,
        compiler_params=pltpu.CompilerParams(
            vmem_limit_bytes=VMEM_LIMIT, collective_id=0, has_side_effects=True
        ),
    )(matrix, grad_out, grad_factor)


def solution(mesh):
    counts = (mesh.shape["rows"], mesh.shape["sub"])
    placed = (P(("rows", "sub"), None), P(("rows", "sub"), None), P())
    return jax.shard_map(
        functools.partial(per_device, counts),
        mesh=mesh,
        in_specs=placed,
        out_specs=P(("rows", "sub"), None),
        check_vma=False,
    )
```

time: 68.6 us -> 55.4 us (0.81)
  Pallas kernels: 66.9 us -> 53.3 us
    pallas_call x1, Pallas kernels: 66.9 us -> 53.3 us  [per_device(): pl.pallas_call(functools.partial(whole_kernel, counts, width), out_shape=...]
where the time goes in v3:
time: 55.4 us; the launch traced here: 55 us
  Pallas kernels  53.3 us (96%)
  local copies, waits for them, and re-layouts  1.62 us (3%)
    pallas_call x1, Pallas kernels, per_device(): pl.pallas_call(functools.partial(whole_kernel, counts, width), out_shape=...  53.3 us
    unnamed x1, local copies, waits for them, and re-layouts  1.62 us

profile of v3, /device:TPU:0, one launch (start us, length us, event | category | flops | bytes accessed | tf_op | source)
XLA Modules:
  0.0 55.0 jit_solution(10915967743859535129)
XLA Ops:
  0.0 53.3 %shard_map.37 = f32[128,384]{1,0:T(8,128)} custom-call(f32[128,384]{1,0:T(8,128)} %matrix_in.1, f32[128,384]{1,0:T(8,128)} %q_grad_in.1, f32[384,384]{1,0:T(8,128)} %grad_factor_in.1), custom_call_target="tpu_custom_call" | custom-call | tf_op jit(solution)/shard_map/pallas_call | solution.py:669
  53.4 1.6 %copy.5 = f32[128,384]{1,0:T(8,128)} copy(f32[128,384]{1,0:T(8,128)} %shard_map.37) | data formatting | bytes 393216

commit v4 on v3

--- a/solution.py
+++ b/solution.py
@@ -178,7 +178,7 @@
             self.total[mine, :] = terms[0]
 
             def send(offset):
-                for core in (1, 0):
+                for core in (0, 1):
                     self.spread(self.peer(offset), core).start()
 
             each_row(self.devices, send)
@@ -501,7 +501,7 @@
     head, rest, later, off, cross = all_sums
     for summer in flat(all_sums):
         summer.bind(row, core, *take(len(summer.scratch())))
-    matrix, q_grad, grad_factor, loads, work, upper1, inverse1, upper2, inverse2, current, held, early = scratch
+    matrix, q_grad, grad_factor, loads, work, upper1, inverse1, upper2, inverse2, current, held, early, gram2, moved, after, turning = scratch
 
     loading = []
     for index, (source, target) in enumerate(
@@ -515,17 +515,17 @@
     line, lane = iotas((LANES, LANES))
     corner = (line == LANES - 1) & (lane == 0)
     head.put(jnp.where(corner, squares, dot6(matrix[:, block(0)], matrix[:, block(0)], TN)))
+    greeted(counts)
+    head.start()
     for b in range(1, width):
         for i in range(b + 1):
             rest[b - 1].put(i, dot6(matrix[:, block(i)], matrix[:, block(b)], TN))
+        rest[b - 1].pair_start()
     loading[1].wait()
     for index, (i, j) in enumerate(pairs):
         cross.put(index, dot6(matrix[:, block(i)], q_grad[:, block(j)], TN))
+    cross.pair_start()
     loading[2].wait()
-    greeted(counts)
-    head.start()
-    for summer in rest + [cross]:
-        summer.pair_start()
     for summer in rest:
         summer.pair_add()
         summer.scatter()
@@ -533,7 +533,6 @@
     head.reduce()
     for summer in rest:
         summer.reduce()
-    cross.scatter()
     head.gathered()
     first_block = head.get(0, LANES)
     shift1 = rate * jnp.broadcast_to(first_block[LANES - 1 : LANES, 0:1], (1, LANES))
@@ -543,67 +542,107 @@
         for summer in rest[1:]:
             summer.share()
 
+    def between_on():
+        for summer in later[1:-1]:
+            summer.pair_add()
+            summer.scatter()
+        later[0].reduce()
+
     def off_on():
-        later[0].reduce()
         off.pair_add()
         off.scatter()
 
-    hooks1 = {0: {2: lambda: rest[0].share()}, 1: {1: rest_share}, last: {1: off_on, 3: cross.share}}
+    def gram1(b):
+        above = jnp.concatenate([rest[b - 1].get(i) for i in range(b)], axis=0)
+        return rest[b - 1].get(b), prepare(b, above, upper1, inverse1)
+
+    hooks1 = {
+        0: {2: rest[0].share},
+        1: {1: rest_share},
+        last: {0: between_on, 1: off_on},
+    }
+    diagonal, prepared = first_block, None
     for b in range(width):
-        if b == 0:
-            diagonal, prepared = first_block, None
-        else:
-            rest[b - 1].shared()
-            above = jnp.concatenate([rest[b - 1].get(i) for i in range(b)], axis=0)
-            diagonal, prepared = rest[b - 1].get(b), prepare(b, above, upper1, inverse1)
         if b == last:
             ahead = matrix[:, block(b)] - dot6(matrix[:, upto(b)], prepared[1], NT)
             for i in range(b):
                 off.put(i, dot6(current[:, block(i)], ahead, TN))
             off.pair_start()
         factor_column(b, diagonal, prepared, shift1, work, upper1, inverse1, hooks1.get(b, {}))
+        if b < last:
+            rest[b].shared()
         current[:, block(b)] = dot6(matrix[:, upto(b + 1)], inverse1[block(b), upto(b + 1)], NT)
-        first = b if b == last else 0
-        later[b].put(dot6(current[:, first * LANES : (b + 1) * LANES], current[:, block(b)], TN))
-        later[b].start()
+        if b in (0, last):
+            later[b].put(dot6(current[:, block(b)], current[:, block(b)], TN))
+        else:
+            for i in range(b + 1):
+                later[b].put(i, dot6(current[:, block(i)], current[:, block(b)], TN))
+        if b < last:
+            diagonal, prepared = gram1(b + 1)
+        if b in (0, last):
+            later[b].start()
+        else:
+            later[b].pair_start()
         if b == 0:
-            cross.reduce()
+            cross.scatter()
     for summer in later[1:-1]:
         summer.reduce()
     inverse = inverse1[...]
     shift2 = rate * (size - shift1 * jnp.sum(inverse * inverse))
-    columns = []
-    for j in range(width):
-        at = j * LANES
-        columns.append(dot3(grad_factor[0 : at + LANES, at:], upper1[at : at + LANES, at:], NT))
-    early[...] = from_columns(width, columns)
-    hooks2 = {0: {1: off.reduce}, 1: {2: off.share}}
-    gram = []
+
+    def early_on():
+        columns = []
+        for j in range(width):
+            at = j * LANES
+            columns.append(dot3(grad_factor[0 : at + LANES, at:], upper1[at : at + LANES, at:], NT))
+        early[...] = from_columns(width, columns)
+
+    def off_above():
+        off.shared()
+        above = jnp.concatenate([off.get(i) for i in range(last)], axis=0)
+        gram2[upto(last), block(last)] = dot6(above, inverse1[block(last), block(last)], NT)
+
+    def cross_on():
+        cross.shared()
+        crossed = [
+            jnp.concatenate([cross.get(pairs.index((i, j))) for j in range(i, width)], axis=1) for i in range(width)
+        ]
+        held[...] = from_rows(width, lower_times_upper(width, inverse1, from_rows(width, crossed), dot6))
+
+    def known_parts():
+        for i in range(last):
+            at = i * LANES
+            moved[at : at + LANES, at:] = dot3(
+                upper2[0 : at + LANES, at : at + LANES], grad_factor[0 : at + LANES, at:], TN
+            )
+        after[:, upto(last)] = dot3(current[:, upto(last)], inverse2[upto(last), upto(last)], NT)
+        turning[:, upto(last)] = dot3(q_grad[:, upto(last)], inverse2[upto(last), upto(last)])
+
+    hooks2 = {
+        0: {1: early_on, 2: off.reduce, 3: cross.reduce},
+        1: {2: off.share, 3: off_above},
+        last: {1: cross.share, 2: known_parts, 3: cross_on},
+    }
     for b in range(width):
         if b == last:
-            off.shared()
-            above = jnp.concatenate([off.get(i) for i in range(b)], axis=0)
-            above = dot6(above, inverse1[block(b), block(b)], NT)
-            prepared = prepare(b, above, upper2, inverse2)
+            prepared = prepare(b, gram2[upto(b), block(b)], upper2, inverse2)
             later[b].gathered()
             diagonal = later[b].get(0, LANES)
-            gram.append(jnp.concatenate([above, diagonal], axis=0))
+            gram2[block(b), block(b)] = diagonal
         else:
-            later[b].gathered()
-            gram.append(later[b].get(0, (b + 1) * LANES))
-            diagonal = gram[b][b * LANES :, :]
-            prepared = prepare(b, gram[b][: b * LANES, :], upper2, inverse2) if b else None
+            if b:
+                later[b].share()
+                later[b].shared()
+                column = jnp.concatenate([later[b].get(i) for i in range(b + 1)], axis=0)
+            else:
+                later[b].gathered()
+                column = later[b].get(0, LANES)
+            gram2[upto(b + 1), block(b)] = column
+            diagonal = column[b * LANES :, :]
+            prepared = prepare(b, column[: b * LANES, :], upper2, inverse2) if b else None
         factor_column(b, diagonal, prepared, shift2, work, upper2, inverse2, hooks2.get(b, {}))
         if b == 0:
             later[-1].reduce()
-            cross.shared()
-            crossed = [
-                jnp.concatenate([cross.get(pairs.index((i, j))) for j in range(i, width)], axis=1)
-                for i in range(width)
-            ]
-            held[...] = from_rows(
-                width, lower_times_upper(width, inverse1, from_rows(width, crossed), dot6)
-            )
 
     row, lane = iotas((size, size))
     inverse = inverse2[...]
@@ -614,7 +653,7 @@
         [dot3(half2[:, j * LANES :], inverse[j * LANES :, j * LANES : (j + 1) * LANES]) for j in range(width)], axis=1
     )
     trace2 = rate * jnp.sum(middle * inverse)
-    gram = from_columns(width, gram)
+    gram = jnp.where(row // LANES <= lane // LANES, gram2[...], 0.0)
     wide2 = jnp.concatenate([shift2] * width, axis=1)
     mixed = upper2[...] - wide2 * inverse
     across = from_columns(
@@ -625,16 +664,18 @@
         ],
     )
     crossed1 = turned + 2.0 * (across + trace2 * gram)
-    moved = []
-    for i in range(width):
-        at = i * LANES
-        moved.append(dot3(upper2[0 : at + LANES, at : at + LANES], grad_factor[0 : at + LANES, at:], TN))
-    total1 = from_rows(width, moved) - from_columns(width, upper_times_lower(width, crossed1, inverse1))
+    moved[block(last), block(last)] = dot3(upper2[:, block(last)], grad_factor[:, block(last)], TN)
+    kept = jnp.where(row // LANES <= lane // LANES, moved[...], 0.0)
+    total1 = kept - from_columns(width, upper_times_lower(width, crossed1, inverse1))
     half1, phi1 = symmetric_half(width, total1, upper1)
     missing = jnp.where(row == lane, 1.0 - gram, -gram)
     trace1 = rate * jnp.sum(phi1 * missing) / shift1
-    after = dot3(current[...], inverse, NT)
-    grad = dot3(q_grad[...], inverse) + 2.0 * (dot3(after, middle) + trace2 * current[...])
+    after[:, block(last)] = dot3(current[...], inverse[last * LANES :, :], NT)
+    turned_grad = dot3(q_grad[:, block(last)], inverse[last * LANES :, :])
+    turned_grad = turned_grad + jnp.concatenate(
+        [turning[:, upto(last)], jnp.zeros((q_grad.shape[0], LANES), jnp.float32)], axis=1
+    )
+    grad = turned_grad + 2.0 * (dot3(after[...], middle) + trace2 * current[...])
     grad = grad + 2.0 * dot3(current[...], half1)
     wide1 = jnp.concatenate([trace1] * width, axis=1)
     out[...] = dot3(grad, inverse1[...]) + 2.0 * wide1 * matrix[...]
@@ -645,7 +686,7 @@
 def summers(counts, width):
     count = width * (width + 1) // 2
     rest = [Paired(counts, (b + 1) * LANES) for b in range(1, width)]
-    later = [Direct(counts, (b + 1) * LANES) for b in range(width - 1)] + [Direct(counts, LANES)]
+    later = [Direct(counts, LANES)] + [Paired(counts, (b + 1) * LANES) for b in range(1, width - 1)] + [Direct(counts, LANES)]
     off = Paired(counts, (width - 1) * LANES)
     return Direct(counts, LANES), rest, later, off, Paired(counts, count * LANES)
 
@@ -665,10 +706,10 @@
     sums = []
     for summer in flat(summers(counts, width)):
         sums = sums + summer.scratch()
-    held = [tall, tall, square, pltpu.SemaphoreType.DMA((3,)), work] + [square] * 4 + [tall, square, square]
+    held = [tall, tall, square, pltpu.SemaphoreType.DMA((3,)), work] + [square] * 4 + [tall, square, square] + [square, square, tall, tall]
     return pl.pallas_call(
         functools.partial(whole_kernel, counts, width),
-        out_shape=jax.ShapeDtypeStruct((rows, size), jnp.float32),
+        out_shape=pltpu.VMEM((rows, size), jnp.float32),
         in_specs=[pl.BlockSpec(memory_space=pl.ANY)] * 3,
         out_specs=vmem,
         scratch_shapes=sums + held,

time: 55.4 us -> 51.4 us (0.928)
  Pallas kernels: 53.3 us -> 50.6 us
  local copies, waits for them, and re-layouts: 1.62 us -> 0.68 us
    pallas_call x1, Pallas kernels: 53.3 us -> 50.6 us  [per_device(): pl.pallas_call(functools.partial(whole_kernel, counts, width), out_shape=...]
    unnamed x1, local copies, waits for them, and re-layouts: 1.62 us -> 0.68 us
where the time goes in v4:
time: 51.4 us; the launch traced here: 51.2 us
  Pallas kernels  50.6 us (98%)
  local copies, waits for them, and re-layouts  0.68 us (1%)
    pallas_call x1, Pallas kernels, per_device(): pl.pallas_call(functools.partial(whole_kernel, counts, width), out_shape=...  50.6 us

profile of v4, /device:TPU:0, one launch (start us, length us, event | category | flops | bytes accessed | tf_op | source)
XLA Modules:
  0.0 51.2 jit_solution(1336148859126560675)
XLA Ops:
  0.0 50.6 %shard_map.37 = f32[128,384]{1,0:T(8,128)S(1)} custom-call(f32[128,384]{1,0:T(8,128)} %matrix_in.1, f32[128,384]{1,0:T(8,128)} %q_grad_in.1, f32[384,384]{1,0:T(8,128)} %grad_factor_in.1), custom_call_target="tpu_custom_call" | custom-call | tf_op jit(solution)/shard_map/pallas_call | solution.py:710
  50.6 0.7 %copy.5 = f32[128,384]{1,0:T(8,128)} copy(f32[128,384]{1,0:T(8,128)S(1)} %shard_map.37) | data formatting | bytes 393216

commit v5 on v4

--- a/solution.py
+++ b/solution.py
@@ -548,6 +548,12 @@
             summer.scatter()
         later[0].reduce()
 
+    def off_start(carried):
+        ahead = matrix[:, block(last)] - dot6(matrix[:, upto(last)], carried, NT)
+        for i in range(last):
+            off.put(i, dot6(current[:, block(i)], ahead, TN))
+        off.pair_start()
+
     def off_on():
         off.pair_add()
         off.scatter()
@@ -559,16 +565,14 @@
     hooks1 = {
         0: {2: rest[0].share},
         1: {1: rest_share},
-        last: {0: between_on, 1: off_on},
+        last: {0: between_on, 3: off_on},
     }
     diagonal, prepared = first_block, None
     for b in range(width):
+        hooks = hooks1.get(b, {})
         if b == last:
-            ahead = matrix[:, block(b)] - dot6(matrix[:, upto(b)], prepared[1], NT)
-            for i in range(b):
-                off.put(i, dot6(current[:, block(i)], ahead, TN))
-            off.pair_start()
-        factor_column(b, diagonal, prepared, shift1, work, upper1, inverse1, hooks1.get(b, {}))
+            hooks = {**hooks, 1: functools.partial(off_start, prepared[1])}
+        factor_column(b, diagonal, prepared, shift1, work, upper1, inverse1, hooks)
         if b < last:
             rest[b].shared()
         current[:, block(b)] = dot6(matrix[:, upto(b + 1)], inverse1[block(b), upto(b + 1)], NT)
@@ -618,10 +622,16 @@
         after[:, upto(last)] = dot3(current[:, upto(last)], inverse2[upto(last), upto(last)], NT)
         turning[:, upto(last)] = dot3(q_grad[:, upto(last)], inverse2[upto(last), upto(last)])
 
+    def later_on():
+        later[-1].reduce()
+        for summer in later[1:-1]:
+            summer.share()
+        cross.reduce()
+
     hooks2 = {
-        0: {1: early_on, 2: off.reduce, 3: cross.reduce},
+        0: {1: early_on, 2: off.reduce, 3: later_on},
         1: {2: off.share, 3: off_above},
-        last: {1: cross.share, 2: known_parts, 3: cross_on},
+        last: {1: known_parts, 2: cross.share, 3: cross_on},
     }
     for b in range(width):
         if b == last:
@@ -631,7 +641,6 @@
             gram2[block(b), block(b)] = diagonal
         else:
             if b:
-                later[b].share()
                 later[b].shared()
                 column = jnp.concatenate([later[b].get(i) for i in range(b + 1)], axis=0)
             else:
@@ -641,9 +650,6 @@
             diagonal = column[b * LANES :, :]
             prepared = prepare(b, column[: b * LANES, :], upper2, inverse2) if b else None
         factor_column(b, diagonal, prepared, shift2, work, upper2, inverse2, hooks2.get(b, {}))
-        if b == 0:
-            later[-1].reduce()
-
     row, lane = iotas((size, size))
     inverse = inverse2[...]
     turned = from_columns(width, upper_times_lower(width, held[...], inverse))

time: 51.4 us -> 50.3 us (0.979)
  Pallas kernels: 50.6 us -> 49.4 us
    pallas_call x1, Pallas kernels: 50.6 us -> 49.4 us  [per_device(): pl.pallas_call(functools.partial(whole_kernel, counts, width), out_shape=...]
where the time goes in v5:
time: 50.3 us; the launch traced here: 50.1 us
  Pallas kernels  49.4 us (98%)
  local copies, waits for them, and re-layouts  0.68 us (1%)
    pallas_call x1, Pallas kernels, per_device(): pl.pallas_call(functools.partial(whole_kernel, counts, width), out_shape=...  49.4 us

profile of v5, /device:TPU:0, one launch (start us, length us, event | category | flops | bytes accessed | tf_op | source)
XLA Modules:
  0.0 50.1 jit_solution(11506333525797389256)
XLA Ops:
  0.0 49.4 %shard_map.37 = f32[128,384]{1,0:T(8,128)S(1)} custom-call(f32[128,384]{1,0:T(8,128)} %matrix_in.1, f32[128,384]{1,0:T(8,128)} %q_grad_in.1, f32[384,384]{1,0:T(8,128)} %grad_factor_in.1), custom_call_target="tpu_custom_call" | custom-call | tf_op jit(solution)/shard_map/pallas_call | solution.py:716
  49.4 0.7 %copy.5 = f32[128,384]{1,0:T(8,128)} copy(f32[128,384]{1,0:T(8,128)S(1)} %shard_map.37) | data formatting | bytes 393216
